TPU v7x, 32 devices: a whole 2x2x4 slice. The times are simulated.
32 devices in a mesh: gx: 4 (over z), gy: 4 (over y, x), gz: 2 (over core).
Axes of the slice: x: 2, y: 2, z: 4, core: 2. Of those that a mesh axis runs over, the one named last changes fastest.
Arguments:
- pair: bfloat16 [128, 128, 128], P('gx', ('gy', 'gz')), may hold values from -6 to 6
- pair_mask: int32 [128, 128], P('gx', ('gy', 'gz')), may hold values 0 or 1
- in_gain: float32 [128], replicated, may hold values from 0.1 to 1.9
- in_bias: float32 [128], replicated, may hold values from -3 to 3
- proj_weight: bfloat16 [128, 512], replicated, may hold values from -0.5 to 0.5
- gate_weight: bfloat16 [128, 128], replicated, may hold values from -0.5 to 0.5
- out_gain: float32 [128], replicated, may hold values from 0.1 to 1.9
- out_bias: float32 [128], replicated, may hold values from -3 to 3
- out_weight: bfloat16 [128, 128], replicated, may hold values from -0.5 to 0.5
Outputs:
- update: bfloat16 [128, 128, 128], P('gx', ('gy', 'gz'))
All inputs are finite; a program needn't handle non-finite values. No bound on the sum of `pair_mask` on one device may be relied on, other than what follows from the above.
Results may differ from a plain program's by a relative error of at most 0.0071.
Values may be sent and summed in bfloat16 or wider, within the bound.
A program may use at most 64 MiB of HBM per device.

v0:
```python
import functools

import jax
import jax.numpy as jnp
from jax import lax
from jax.experimental import pallas as pl
from jax.experimental.pallas import tpu as pltpu
from jax.sharding import PartitionSpec as P

MESH = pl.DeviceIdType.MESH
LANES = 128
EPSILON = 1e-05
PARTS = 2
RIGHT_STEPS = 2
TRI_STEPS = 1


def normalize(values, gain, bias):
    average = jnp.mean(values, axis=-1, keepdims=True)
    centered = values - average
    variance = jnp.mean(centered * centered, axis=-1, keepdims=True)
    return centered * lax.rsqrt(variance + EPSILON) * gain + bias


def project(tile, mask_value, in_gain, in_bias, proj_weight):
    hidden = proj_weight.shape[1] // 4
    normed = normalize(tile.astype(jnp.float32), in_gain, in_bias).astype(jnp.bfloat16)
    projected = jnp.einsum("rwc,cd->rwd", normed, proj_weight, preferred_element_type=jnp.float32)
    left_side = (
        jax.nn.sigmoid(projected[:, :, :hidden]) * projected[:, :, hidden : 2 * hidden] * mask_value
    ).astype(jnp.bfloat16)
    right_side = (
        jax.nn.sigmoid(projected[:, :, 2 * hidden : 3 * hidden])
        * projected[:, :, 3 * hidden :]
        * mask_value
    ).astype(jnp.bfloat16)
    return (normed, left_side, right_side)


def with_collectives(
    pair, pair_mask, in_gain, in_bias, proj_weight, gate_weight, out_gain, out_bias, out_weight
):
    mask_value = pair_mask.astype(jnp.float32)[:, :, None]
    normed, left_side, own_right = project(pair, mask_value, in_gain, in_bias, proj_weight)
    left_slab, right_slab = (
        lax.all_gather(left_side, "gy", axis=1, tiled=True),
        lax.all_gather(own_right, "gy", axis=1, tiled=True),
    )
    every_row = lax.all_gather(own_right, "gx", axis=0, tiled=True)
    row_panel = lax.all_to_all(every_row, "gy", split_axis=0, concat_axis=1, tiled=True)
    summed = lax.psum_scatter(
        jnp.einsum("jkc,ikc->jic", row_panel, left_slab, preferred_element_type=jnp.float32),
        "gz",
        scatter_dimension=0,
        tiled=True,
    )
    triangle = jnp.transpose(summed, (1, 0, 2))
    tri_normed = normalize(triangle, out_gain, out_bias).astype(jnp.bfloat16)
    gating = jax.nn.sigmoid(
        jnp.einsum("rwc,cd->rwd", normed, gate_weight, preferred_element_type=jnp.float32)
    )
    mixed = jnp.einsum("rwh,hc->rwc", tri_normed, out_weight, preferred_element_type=jnp.float32)
    return (gating * mixed).astype(jnp.bfloat16)


def swap_groups(tiles, width):
    tiles = list(tiles)
    group = lax.broadcasted_iota(jnp.int32, tiles[0].shape, 1) // width
    bit = 1
    while bit < len(tiles):
        upper = (group // bit) % 2 == 1
        for a in range(len(tiles)):
            if (a // bit) % 2 == 0:
                low, high = tiles[a], tiles[a + bit]
                tiles[a] = jnp.where(upper, pltpu.roll(high, bit * width, 1), low)
                tiles[a + bit] = jnp.where(upper, high, pltpu.roll(low, LANES - bit * width, 1))
        bit *= 2
    return tiles


def kernel(
    nx,
    ny,
    nz,
    pair_hbm,
    mask_hbm,
    in_gain_hbm,
    in_bias_hbm,
    proj_hbm,
    gate_hbm,
    out_gain_hbm,
    out_bias_hbm,
    out_weight_hbm,
    out_ref,
    right_out,
    left_out,
    tri_out,
    right_in,
    left_in,
    tri_in,
    right_all,
    left_all,
    left_far,
    tri_far,
    spread,
    normed_ref,
    gating_ref,
    right_sems,
    left_sems,
    tri_sems,
    z_send,
    z_recv,
    far_sems,
    far_send,
    pair_ref,
    mask_ref,
    in_gain_ref,
    in_bias_ref,
    proj_ref,
    gate_ref,
    out_gain_ref,
    out_bias_ref,
    out_weight_ref,
    load_sems,
):
    rows, width, channels = pair_ref.shape
    hidden = proj_ref.shape[1] // 4
    plane = ny * nz
    block = hidden // plane
    tiles = rows * width // LANES
    per_tile = rows // tiles
    per_step = tiles // TRI_STEPS
    part = block // PARTS
    x, y, z = lax.axis_index("gx"), lax.axis_index("gy"), lax.axis_index("gz")
    me = y * nz + z
    owners = rows // width
    is_end = jnp.logical_or(x == 0, x == nx - 1)
    is_helper = jnp.logical_or(x == 1, x == nx - 2)
    end = jnp.where(x < nx // 2, 0, nx - 1)
    helper = jnp.where(x < nx // 2, 1, nx - 2)

    def is_left_out(d):
        return jnp.logical_and(is_end, d // owners == nx - 1 - end)


    def peer(t):
        d = lax.rem(me + t, plane)
        return d, (x, d // nz, lax.rem(d, nz))

    arguments = (
        (pair_hbm, pair_ref),
        (mask_hbm, mask_ref),
        (in_gain_hbm, in_gain_ref),
        (in_bias_hbm, in_bias_ref),
        (proj_hbm, proj_ref),
        (gate_hbm, gate_ref),
        (out_gain_hbm, out_gain_ref),
        (out_bias_hbm, out_bias_ref),
        (out_weight_hbm, out_weight_ref),
    )
    loads = [
        pltpu.make_async_copy(held, wanted, load_sems.at[index])
        for index, (held, wanted) in enumerate(arguments)
    ]
    for load in loads:
        load.start()
    barrier = pltpu.get_barrier_semaphore()
    for t in range(1, plane):
        pl.semaphore_signal(barrier, inc=1, device_id=peer(t)[1], device_id_type=MESH)

    @pl.when(x > 0)
    def _():
        pl.semaphore_signal(barrier, inc=1, device_id=(x - 1, y, z), device_id_type=MESH)

    @pl.when(x < nx - 1)
    def _():
        pl.semaphore_signal(barrier, inc=1, device_id=(x + 1, y, z), device_id_type=MESH)

    @pl.when(is_left_out(me))
    def _():
        for t in range(plane):
            d = lax.rem(me + t, plane)
            device = (helper, d // nz, lax.rem(d, nz))
            pl.semaphore_signal(barrier, inc=1, device_id=device, device_id_type=MESH)

    for load in (loads[0], loads[2], loads[3]):
        load.wait()

    def norm(step):
        some = slice(step * rows // RIGHT_STEPS, (step + 1) * rows // RIGHT_STEPS)
        pairs = slice(some.start * width, some.stop * width)
        normed_ref[pairs, :] = normalize(
            pair_ref[some].reshape(-1, channels).astype(jnp.float32), in_gain_ref[...], in_bias_ref[...]
        ).astype(jnp.bfloat16)

    norm(0)

    loads[1].wait()
    row_of = lax.broadcasted_iota(jnp.int32, (rows, rows * width), 1) // width
    choose = (row_of == lax.broadcasted_iota(jnp.int32, row_of.shape, 0)).astype(jnp.bfloat16)
    repeated = jnp.dot(
        mask_ref[...].astype(jnp.float32).astype(jnp.bfloat16), choose, preferred_element_type=jnp.float32
    )
    column_of = lax.broadcasted_iota(jnp.int32, repeated.shape, 1) % width
    own_column = column_of == lax.broadcasted_iota(jnp.int32, repeated.shape, 0)
    mask_row = jnp.sum(jnp.where(own_column, repeated, 0.0), axis=0, keepdims=True)

    def side(weight, target, step, steps):
        for q in range(step * tiles // steps, (step + 1) * tiles // steps):
            lanes = slice(q * LANES, (q + 1) * LANES)
            projected = lax.dot_general(
                weight, normed_ref[lanes, :], (((1,), (1,)), ((), ())), preferred_element_type=jnp.float32
            )
            value = jax.nn.sigmoid(projected[:hidden]) * projected[hidden:] * mask_row[:, lanes]
            target[:, q] = value.astype(jnp.bfloat16).reshape(plane, block, LANES)

    def exchange(source, target, sems, step, steps):
        count = tiles // steps
        copies = []
        for t in range(1, plane):
            d, device = peer(t)
            copies.append(
                pltpu.make_async_remote_copy(
                    src_ref=source.at[d, pl.ds(step * count, count)],
                    dst_ref=target.at[me, pl.ds(step * count, count)],
                    send_sem=sems.at[0, step, t],
                    recv_sem=sems.at[1, step, t],
                    device_id=device,
                    device_id_type=MESH,
                )
            )
            copies[-1].start()
        target[me, step * count : (step + 1) * count] = source[me, step * count : (step + 1) * count]
        return copies

    def gather_sums(source, target, step, steps):
        some = rows // steps
        for index, q in enumerate(range(step * tiles // steps, (step + 1) * tiles // steps)):
            swapped = swap_groups([source[a, q].astype(jnp.float32) for a in range(plane)], width)
            for a in range(per_tile):
                first = step * some * block + index * per_tile + a
                spread[pl.ds(first, block, stride=some), :] = swapped[a]
        target[:, step * some : (step + 1) * some] = (
            spread[step * some * block : (step + 1) * some * block]
            .astype(jnp.bfloat16)
            .reshape(block, some, LANES)
        )

    loads[4].wait()
    right_weight = proj_ref[:, 2 * hidden :].T
    right_copies = []
    for step in range(RIGHT_STEPS):
        if step > 0:
            norm(step)
        side(right_weight, right_out, step, RIGHT_STEPS)
        if step == 0:
            pl.semaphore_wait(
                barrier, jnp.where(is_end, plane, jnp.where(is_helper, plane + 1 + owners, plane + 1))
            )
        right_copies.append(exchange(right_out, right_in, right_sems, step, RIGHT_STEPS))
    side(proj_ref[:, : 2 * hidden].T, left_out, 0, 1)
    left_copies = exchange(left_out, left_in, left_sems, 0, 1)
    loads[5].wait()
    gating_ref[...] = jax.nn.sigmoid(
        jnp.dot(normed_ref[...], gate_ref[...], preferred_element_type=jnp.float32)
    )

    pieces = RIGHT_STEPS * PARTS

    def piece_of(origin, piece):
        some = rows // RIGHT_STEPS
        return right_all.at[
            origin, pl.ds(piece % PARTS * part, part), pl.ds(piece // PARTS * some, some)
        ]

    def pass_on(way, t, piece):
        ahead = x + 1 if way == 0 else x - 1
        origin = x - t if way == 0 else x + t
        part_of = piece_of(origin, piece)
        return pltpu.make_async_remote_copy(
            src_ref=part_of,
            dst_ref=part_of,
            send_sem=z_send.at[way, t, piece],
            recv_sem=z_recv.at[way, t, piece],
            device_id=(ahead, y, z),
            device_id_type=MESH,
        )

    def has_ahead(way):
        return x < nx - 1 if way == 0 else x > 0

    def has_origin(way, t):
        return x >= t if way == 0 else x <= nx - 1 - t

    for step in range(RIGHT_STEPS):
        for copy in right_copies[step]:
            copy.wait_recv()
        gather_sums(right_in, right_all.at[x], step, RIGHT_STEPS)
        for piece in range(step * PARTS, (step + 1) * PARTS):
            for way in range(2):

                @pl.when(has_ahead(way))
                def _():
                    pass_on(way, 0, piece).start()

    for copy in left_copies:
        copy.wait_recv()
    gather_sums(left_in, left_all, 0, 1)

    left_copy = pltpu.make_async_remote_copy(
        src_ref=left_all,
        dst_ref=left_far,
        send_sem=far_sems.at[0],
        recv_sem=far_sems.at[1],
        device_id=(helper, y, z),
        device_id_type=MESH,
    )

    @pl.when(is_end)
    def _():
        left_copy.start()
        right_all[nx - 1 - end] = jnp.zeros(right_all.shape[1:], right_all.dtype)

    for t in range(1, nx - 1):
        for piece in range(pieces):
            for way in range(2):

                @pl.when(has_origin(way, t))
                def _():
                    pltpu.make_async_remote_copy(
                        src_ref=piece_of(x, piece),
                        dst_ref=piece_of(x - t if way == 0 else x + t, piece),
                        send_sem=z_send.at[way, t - 1, piece],
                        recv_sem=z_recv.at[way, t - 1, piece],
                        device_id=(x, y, z),
                        device_id_type=MESH,
                    ).wait_recv()
                    if t < nx - 2:

                        @pl.when(has_ahead(way))
                        def _():
                            pass_on(way, t, piece).start()

    def multiply(left, target, send):
        for c in range(block):
            triangle = lax.dot_general(
                left[c],
                right_all[:, c].reshape(nx * rows, LANES),
                (((1,), (1,)), ((), ())),
                preferred_element_type=jnp.float32,
            )
            spread[pl.ds(c, rows, stride=block), :] = triangle
        for q in range(tiles):
            swapped = swap_groups(
                [spread[pl.ds((q * per_tile + a) * block, block), :] for a in range(per_tile)], width
            )
            for d in range(plane):
                target[d, q] = swapped[d].astype(jnp.bfloat16)
            if (q + 1) % per_step == 0:
                send(q // per_step)

    def far_copy(index, step):
        d = (nx - 1 - end) * owners + index
        return pltpu.make_async_remote_copy(
            src_ref=tri_far.at[d, pl.ds(step * per_step, per_step)],
            dst_ref=tri_in.at[me, pl.ds(step * per_step, per_step)],
            send_sem=far_send.at[step, index],
            recv_sem=tri_sems.at[1, step, lax.rem(d - me + plane, plane)],
            device_id=(end, d // nz, lax.rem(d, nz)),
            device_id_type=MESH,
        )

    def tri_copy(t, step):
        d, device = peer(t)
        return pltpu.make_async_remote_copy(
            src_ref=tri_out.at[d, pl.ds(step * per_step, per_step)],
            dst_ref=tri_in.at[me, pl.ds(step * per_step, per_step)],
            send_sem=tri_sems.at[0, step, t],
            recv_sem=tri_sems.at[1, step, t],
            device_id=device,
            device_id_type=MESH,
        )

    def send_far(step):
        for index in range(owners):
            far_copy(index, step).start()

    def send(step):
        for t in range(1, plane):

            @pl.when(jnp.logical_not(is_left_out(peer(t)[0])))
            def _():
                tri_copy(t, step).start()

    def receive(step):
        @pl.when(is_left_out(me))
        def _():
            tri_copy(0, step).wait_recv()

        for t in range(1, plane):
            tri_copy(t, step).wait_recv()

    @pl.when(is_helper)
    def _():
        left_copy.wait_recv()
        multiply(left_far, tri_far, send_far)

    multiply(left_all, tri_out, send)

    @pl.when(jnp.logical_not(is_left_out(me)))
    def _():
        tri_in[me] = tri_out[me]

    for load in loads[6:]:
        load.wait()
    for q in range(tiles):
        if q % per_step == 0:
            receive(q // per_step)
        lanes = slice(q * LANES, (q + 1) * LANES)
        sums = tri_in[:, q].reshape(hidden, LANES).astype(jnp.float32)
        centered = sums - jnp.mean(sums, axis=0, keepdims=True)
        variance = jnp.mean(centered * centered, axis=0, keepdims=True)
        scaled = (centered * lax.rsqrt(variance + EPSILON)).T
        tri_normed = (scaled * out_gain_ref[...] + out_bias_ref[...]).astype(jnp.bfloat16)
        mixed = jnp.dot(tri_normed, out_weight_ref[...], preferred_element_type=jnp.float32)
        out_ref[q * per_tile : (q + 1) * per_tile] = (
            (gating_ref[lanes, :] * mixed).astype(jnp.bfloat16).reshape(per_tile, width, channels)
        )

    for copy in sum(right_copies, left_copies):
        copy.wait_send()
    for t in range(1, plane):

        @pl.when(jnp.logical_not(is_left_out(peer(t)[0])))
        def _():
            for step in range(TRI_STEPS):
                tri_copy(t, step).wait_send()

    @pl.when(is_helper)
    def _():
        for index in range(owners):
            for step in range(TRI_STEPS):
                far_copy(index, step).wait_send()

    @pl.when(is_end)
    def _():
        left_copy.wait_send()

    for t in range(nx - 2):
        for piece in range(pieces):
            for way in range(2):

                @pl.when(jnp.logical_and(has_ahead(way), has_origin(way, t)))
                def _():
                    pass_on(way, t, piece).wait_send()


def fused(nx, ny, nz, *arguments):
    pair, pair_mask, in_gain, in_bias, proj_weight, gate_weight, out_gain, out_bias, out_weight = arguments
    rows, width, channels = pair.shape
    hidden = proj_weight.shape[1] // 4
    plane = ny * nz
    block = hidden // plane
    tiles = rows * width // LANES
    travelling = pltpu.VMEM((plane, tiles, block, LANES), jnp.bfloat16)
    return pl.pallas_call(
        functools.partial(kernel, nx, ny, nz),
        out_shape=jax.ShapeDtypeStruct(pair.shape, jnp.bfloat16),
        in_specs=[pl.BlockSpec(memory_space=pltpu.HBM)] * 9,
        out_specs=pl.BlockSpec(memory_space=pltpu.VMEM),
        scratch_shapes=[travelling] * 6
        + [
            pltpu.VMEM((nx, block, rows, LANES), jnp.bfloat16),
            pltpu.VMEM((block, rows, LANES), jnp.bfloat16),
            pltpu.VMEM((block, rows, LANES), jnp.bfloat16),
            travelling,
            pltpu.VMEM((block * rows, LANES), jnp.float32),
            pltpu.VMEM((rows * width, channels), jnp.bfloat16),
            pltpu.VMEM((rows * width, channels), jnp.float32),
        ]
        + [pltpu.SemaphoreType.DMA((2, steps, plane)) for steps in (RIGHT_STEPS, 1, TRI_STEPS)]
        + [pltpu.SemaphoreType.DMA((2, nx - 2, RIGHT_STEPS * PARTS))] * 2
        + [pltpu.SemaphoreType.DMA((2,)), pltpu.SemaphoreType.DMA((TRI_STEPS, rows // width))]
        + [
            pltpu.VMEM(pair.shape, pair.dtype),
            pltpu.VMEM((width, rows), pair_mask.dtype),
            pltpu.VMEM((1, in_gain.size), in_gain.dtype),
            pltpu.VMEM((1, in_bias.size), in_bias.dtype),
            pltpu.VMEM(proj_weight.shape, proj_weight.dtype),
            pltpu.VMEM(gate_weight.shape, gate_weight.dtype),
            pltpu.VMEM((1, out_gain.size), out_gain.dtype),
            pltpu.VMEM((1, out_bias.size), out_bias.dtype),
            pltpu.VMEM(out_weight.shape, out_weight.dtype),
            pltpu.SemaphoreType.DMA((9,)),
        ],
        compiler_params=pltpu.CompilerParams(collective_id=0, has_side_effects=True),
    )(
        pair,
        pair_mask.T,
        in_gain.reshape(1, -1),
        in_bias.reshape(1, -1),
        proj_weight,
        gate_weight,
        out_gain.reshape(1, -1),
        out_bias.reshape(1, -1),
        out_weight,
    )


def solution(mesh):
    nx, ny, nz = mesh.shape["gx"], mesh.shape["gy"], mesh.shape["gz"]
    plane = ny * nz

    def on_device(pair, *others):
        rows, width, channels = pair.shape
        hidden = others[3].shape[1] // 4
        fits = (
            width * plane == LANES
            and rows * nx == LANES
            and rows % plane == 0
            and rows % width == 0
            and rows * width % (RIGHT_STEPS * TRI_STEPS * LANES) == 0
            and nx >= 4
            and channels % LANES == 0
            and hidden % (16 * plane) == 0
        )
        if fits:
            return fused(nx, ny, nz, pair, *others)
        return with_collectives(pair, *others)

    return jax.shard_map(
        on_device,
        mesh=mesh,
        in_specs=(
            P("gx", ("gy", "gz"), None),
            P("gx", ("gy", "gz")),
            P(),
            P(),
            P(),
            P(),
            P(),
            P(),
            P(),
        ),
        out_specs=P("gx", ("gy", "gz"), None),
        check_vma=False,
    )
```

profile of v0, /device:TPU:0, one launch (start us, length us, event | category | flops | bytes accessed | tf_op | source)
XLA Modules:
  0.0 24.0 jit_solution(1502020927091332494)
XLA Ops:
  0.0 22.4 %shard_map.91 = bf16[32,16,128]{2,1,0:T(8,128)(2,1)} custom-call(bf16[32,16,128]{2,1,0:T(8,128)(2,1)} %pair_hbm.1, s32[16,32]{1,0:T(8,128)} %bitcast.5, f32[1,128]{1,0:T(1,128)} %bitcast.6, f32[1,128]{1,0:T(1,128)} %bitcast.7, bf16[128,512]{1,0:T(8,128)(2,1)} %proj_hbm.1, bf16[128,128]{1,0:T(8,128)(2,1)} %gate_hbm.1, f32[1,128]{1,0:T(1,128)} %bitcast.8, ...), custom_call_target="tpu_custom_call" | custom-call | tf_op jit(solution)/shard_map/pallas_call | solution.py:466
  22.4 1.6 %copy.11 = bf16[32,16,128]{2,1,0:T(8,128)(2,1)} copy(bf16[32,16,128]{2,1,0:T(8,128)(2,1)} %shard_map.91) | data formatting | bytes 262144
where the time goes:
time: 24.1 us; the launch traced here: 24 us
  Pallas kernels  22.4 us (93%)
  local copies, waits for them, and re-layouts  1.57 us (7%)
    pallas_call x1, Pallas kernels, fused(): pl.pallas_call(functools.partial(kernel, nx, ny, nz), out_shape=jax.Shape...  22.4 us
    unnamed x1, local copies, waits for them, and re-layouts  1.57 us

commit v1 on v0

--- a/solution.py
+++ b/solution.py
@@ -465,7 +465,7 @@
     travelling = pltpu.VMEM((plane, tiles, block, LANES), jnp.bfloat16)
     return pl.pallas_call(
         functools.partial(kernel, nx, ny, nz),
-        out_shape=jax.ShapeDtypeStruct(pair.shape, jnp.bfloat16),
+        out_shape=pltpu.VMEM(pair.shape, jnp.bfloat16),
         in_specs=[pl.BlockSpec(memory_space=pltpu.HBM)] * 9,
         out_specs=pl.BlockSpec(memory_space=pltpu.VMEM),
         scratch_shapes=[travelling] * 6

time: 24.1 us -> 22.6 us (0.938)
  local copies, waits for them, and re-layouts: 1.57 us -> 0.66 us
  Pallas kernels: 22.4 us -> 21.7 us
    unnamed x1, local copies, waits for them, and re-layouts: 1.57 us -> 0.66 us
    pallas_call x1, Pallas kernels: 22.4 us -> 21.7 us  [fused(): pl.pallas_call(functools.partial(kernel, nx, ny, nz), out_shape=pltpu.VME...]
where the time goes in v1:
time: 22.6 us; the launch traced here: 22.4 us
  Pallas kernels  21.7 us (96%)
  local copies, waits for them, and re-layouts  0.66 us (3%)
    pallas_call x1, Pallas kernels, fused(): pl.pallas_call(functools.partial(kernel, nx, ny, nz), out_shape=pltpu.VME...  21.7 us
    unnamed x1, local copies, waits for them, and re-layouts  0.66 us

profile of v1, /device:TPU:0, one launch (start us, length us, event | category | flops | bytes accessed | tf_op | source)
XLA Modules:
  0.0 22.4 jit_solution(7861632118219895018)
XLA Ops:
  0.0 21.7 %shard_map.91 = bf16[32,16,128]{2,1,0:T(8,128)(2,1)S(1)} custom-call(bf16[32,16,128]{2,1,0:T(8,128)(2,1)} %pair_hbm.1, s32[16,32]{1,0:T(8,128)} %bitcast.5, f32[1,128]{1,0:T(1,128)} %bitcast.6, f32[1,128]{1,0:T(1,128)} %bitcast.7, bf16[128,512]{1,0:T(8,128)(2,1)} %proj_hbm.1, bf16[128,128]{1,0:T(8,128)(2,1)} %gate_hbm.1, f32[1,128]{1,0:T(1,128)} %bitcast.8, ...), custom_call_target="tpu_custom_call" | custom-call | tf_op jit(solution)/shard_map/pallas_call | solution.py:466
  21.7 0.7 %copy.11 = bf16[32,16,128]{2,1,0:T(8,128)(2,1)} copy(bf16[32,16,128]{2,1,0:T(8,128)(2,1)S(1)} %shard_map.91) | data formatting | bytes 262144

commit v2 on v1

v2 whole, which is shorter than its diff:
```python
import functools

import jax
import jax.numpy as jnp
from jax import lax
from jax.experimental import pallas as pl
from jax.experimental.pallas import tpu as pltpu
from jax.sharding import PartitionSpec as P

MESH = pl.DeviceIdType.MESH
LANES = 128
EPSILON = 1e-05
RIGHT_STEPS = 2
PAD = 1


def normalize(values, gain, bias):
    average = jnp.mean(values, axis=-1, keepdims=True)
    centered = values - average
    variance = jnp.mean(centered * centered, axis=-1, keepdims=True)
    return centered * lax.rsqrt(variance + EPSILON) * gain + bias


def project(tile, mask_value, in_gain, in_bias, proj_weight):
    hidden = proj_weight.shape[1] // 4
    normed = normalize(tile.astype(jnp.float32), in_gain, in_bias).astype(jnp.bfloat16)
    projected = jnp.einsum("rwc,cd->rwd", normed, proj_weight, preferred_element_type=jnp.float32)
    left_side = (
        jax.nn.sigmoid(projected[:, :, :hidden]) * projected[:, :, hidden : 2 * hidden] * mask_value
    ).astype(jnp.bfloat16)
    right_side = (
        jax.nn.sigmoid(projected[:, :, 2 * hidden : 3 * hidden])
        * projected[:, :, 3 * hidden :]
        * mask_value
    ).astype(jnp.bfloat16)
    return (normed, left_side, right_side)


def with_collectives(
    pair, pair_mask, in_gain, in_bias, proj_weight, gate_weight, out_gain, out_bias, out_weight
):
    mask_value = pair_mask.astype(jnp.float32)[:, :, None]
    normed, left_side, own_right = project(pair, mask_value, in_gain, in_bias, proj_weight)
    left_slab, right_slab = (
        lax.all_gather(left_side, "gy", axis=1, tiled=True),
        lax.all_gather(own_right, "gy", axis=1, tiled=True),
    )
    every_row = lax.all_gather(own_right, "gx", axis=0, tiled=True)
    row_panel = lax.all_to_all(every_row, "gy", split_axis=0, concat_axis=1, tiled=True)
    summed = lax.psum_scatter(
        jnp.einsum("jkc,ikc->jic", row_panel, left_slab, preferred_element_type=jnp.float32),
        "gz",
        scatter_dimension=0,
        tiled=True,
    )
    triangle = jnp.transpose(summed, (1, 0, 2))
    tri_normed = normalize(triangle, out_gain, out_bias).astype(jnp.bfloat16)
    gating = jax.nn.sigmoid(
        jnp.einsum("rwc,cd->rwd", normed, gate_weight, preferred_element_type=jnp.float32)
    )
    mixed = jnp.einsum("rwh,hc->rwc", tri_normed, out_weight, preferred_element_type=jnp.float32)
    return (gating * mixed).astype(jnp.bfloat16)


def swap_groups(tiles, width):
    tiles = list(tiles)
    group = lax.broadcasted_iota(jnp.int32, tiles[0].shape, 1) // width
    bit = 1
    while bit < len(tiles):
        upper = (group // bit) % 2 == 1
        for a in range(len(tiles)):
            if (a // bit) % 2 == 0:
                low, high = tiles[a], tiles[a + bit]
                tiles[a] = jnp.where(upper, pltpu.roll(high, bit * width, 1), low)
                tiles[a + bit] = jnp.where(upper, high, pltpu.roll(low, LANES - bit * width, 1))
        bit *= 2
    return tiles


def kernel(
    nx,
    ny,
    nz,
    pair_hbm,
    mask_hbm,
    in_gain_hbm,
    in_bias_hbm,
    proj_hbm,
    gate_hbm,
    out_gain_hbm,
    out_bias_hbm,
    out_weight_hbm,
    out_ref,
    right_out,
    left_out,
    tri_out,
    right_in,
    left_in,
    tri_in,
    right_all,
    left_all,
    spread,
    normed_ref,
    gating_ref,
    right_send,
    right_recv,
    left_send,
    left_recv,
    tri_send,
    tri_recv,
    pair_ref,
    mask_ref,
    in_gain_ref,
    in_bias_ref,
    proj_ref,
    gate_ref,
    out_gain_ref,
    out_bias_ref,
    out_weight_ref,
    load_sems,
):
    rows, width, channels = pair_ref.shape
    hidden = proj_ref.shape[1] // 4
    plane = ny * nz
    block = hidden // plane
    tiles = rows * width // LANES
    per_tile = rows // tiles
    half = nx // 2
    owners = half * rows // width
    x, y, z = lax.axis_index("gx"), lax.axis_index("gy"), lax.axis_index("gz")
    me = y * nz + z
    last = nx - 1
    is_inner = jnp.logical_or(x == half - 1, x == half)
    beside = x + 1 - 2 * lax.rem(x, 2)
    across = jnp.where(x < half, half, half - 1)
    near = jnp.where(is_inner, beside, x)
    slot = lax.rem(x, 2)
    slot_beside = lax.rem(beside, 2)
    first = lax.rem(x, 2) * half
    owner0 = (x // half) * owners
    holds_left = near == x
    sums_here = (me // owners) * half + x // half == x

    def at(row, d):
        return (row, d // nz, lax.rem(d, nz))

    def turn(t):
        return lax.rem(me + t, plane)

    arguments = (
        (pair_hbm, pair_ref),
        (mask_hbm, mask_ref),
        (in_gain_hbm, in_gain_ref),
        (in_bias_hbm, in_bias_ref),
        (proj_hbm, proj_ref),
        (gate_hbm, gate_ref),
        (out_gain_hbm, out_gain_ref),
        (out_bias_hbm, out_bias_ref),
        (out_weight_hbm, out_weight_ref),
    )
    loads = [
        pltpu.make_async_copy(held, wanted, load_sems.at[index])
        for index, (held, wanted) in enumerate(arguments)
    ]
    for load in loads:
        load.start()
    barrier = pltpu.get_barrier_semaphore()

    def greet(row, start):
        for t in range(start, plane):
            pl.semaphore_signal(barrier, inc=1, device_id=at(row, turn(t)), device_id_type=MESH)

    @pl.when(is_inner)
    def _():
        greet(across, 0)
        greet(jnp.where(x < half, last, 0), 0)

    greet(beside, 0)
    greet(x, 1)

    for load in (loads[0], loads[2], loads[3]):
        load.wait()

    def norm(step):
        some = slice(step * rows // RIGHT_STEPS, (step + 1) * rows // RIGHT_STEPS)
        pairs = slice(some.start * width, some.stop * width)
        normed_ref[pairs, :] = normalize(
            pair_ref[some].reshape(-1, channels).astype(jnp.float32), in_gain_ref[...], in_bias_ref[...]
        ).astype(jnp.bfloat16)

    norm(0)

    loads[1].wait()
    row_of = lax.broadcasted_iota(jnp.int32, (rows, rows * width), 1) // width
    choose = (row_of == lax.broadcasted_iota(jnp.int32, row_of.shape, 0)).astype(jnp.bfloat16)
    repeated = jnp.dot(
        mask_ref[...].astype(jnp.float32).astype(jnp.bfloat16), choose, preferred_element_type=jnp.float32
    )
    column_of = lax.broadcasted_iota(jnp.int32, repeated.shape, 1) % width
    own_column = column_of == lax.broadcasted_iota(jnp.int32, repeated.shape, 0)
    mask_row = jnp.sum(jnp.where(own_column, repeated, 0.0), axis=0, keepdims=True)

    def side(weight, target, step, steps):
        for q in range(step * tiles // steps, (step + 1) * tiles // steps):
            lanes = slice(q * LANES, (q + 1) * LANES)
            projected = lax.dot_general(
                weight, normed_ref[lanes, :], (((1,), (1,)), ((), ())), preferred_element_type=jnp.float32
            )
            value = jax.nn.sigmoid(projected[:hidden]) * projected[hidden:] * mask_row[:, lanes]
            target[:, q] = value.astype(jnp.bfloat16).reshape(plane, block, LANES)

    def part_of(step, steps):
        return pl.ds(step * tiles // steps, tiles // steps)

    def right_copy(far, step, t):
        d = turn(t)
        return pltpu.make_async_remote_copy(
            src_ref=right_out.at[d, part_of(step, RIGHT_STEPS)],
            dst_ref=right_in.at[slot, me, part_of(step, RIGHT_STEPS)],
            send_sem=right_send.at[far],
            recv_sem=right_recv.at[slot],
            device_id=at(beside if far else x, d),
            device_id_type=MESH,
        )

    def left_copy(far, t):
        d = turn(t)
        return pltpu.make_async_remote_copy(
            src_ref=left_out.at[d],
            dst_ref=left_in.at[slot, me],
            send_sem=left_send.at[far],
            recv_sem=left_recv.at[slot],
            device_id=at(across if far else near, d),
            device_id_type=MESH,
        )

    def all_of(held, number, target, send_sem, recv_sem):
        return pltpu.make_async_remote_copy(
            src_ref=held.at[pl.ds(0, number)],
            dst_ref=target.at[pl.ds(0, number)],
            send_sem=send_sem,
            recv_sem=recv_sem,
            device_id=at(beside, me),
            device_id_type=MESH,
        )

    def all_right(which, far, number):
        return all_of(right_out, number, right_in.at[which], right_send.at[far], right_recv.at[which])

    def all_left(which, far, number):
        return all_of(left_out, number, left_in.at[which], left_send.at[far], left_recv.at[which])

    def send_right(far):
        for step in range(RIGHT_STEPS):
            for t in range(0 if far else 1, plane):
                right_copy(far, step, t).start()

    def send_left(far):
        for t in range(1, plane):
            left_copy(far, t).start()
        if far:
            left_copy(far, 0).start()
        else:

            @pl.when(jnp.logical_not(holds_left))
            def _():
                left_copy(far, 0).start()

    def all_greeted():
        pl.semaphore_wait(barrier, 3 * plane - 1)

    loads[4].wait()
    right_weight = proj_ref[:, 2 * hidden :].T
    for step in range(RIGHT_STEPS):
        if step > 0:
            norm(step)
        side(right_weight, right_out, step, RIGHT_STEPS)

    @pl.when(x == last)
    def _():
        all_greeted()
        send_right(1)

    side(proj_ref[:, : 2 * hidden].T, left_out, 0, 1)

    @pl.when(x != last)
    def _():
        all_greeted()

    @pl.when(x == half)
    def _():
        send_right(0)

    send_left(1)

    @pl.when(x != last)
    def _():
        send_right(1)

    @pl.when(x != half)
    def _():
        send_right(0)

    send_left(0)
    right_in[slot, me] = right_out[me]

    @pl.when(holds_left)
    def _():
        left_in[slot, me] = left_out[me]

    loads[5].wait()
    gating_ref[...] = jax.nn.sigmoid(
        jnp.dot(normed_ref[...], gate_ref[...], preferred_element_type=jnp.float32)
    )

    def gather_sums(source, target, step, steps):
        some = rows // steps
        for index, q in enumerate(range(step * tiles // steps, (step + 1) * tiles // steps)):
            swapped = swap_groups([source[a, q].astype(jnp.float32) for a in range(plane)], width)
            for a in range(per_tile):
                spread[pl.ds(index * per_tile + a, block, stride=some + PAD), :] = swapped[a]
        for c in range(block):
            target[c, step * some : (step + 1) * some] = spread[
                pl.ds(c * (some + PAD), some), :
            ].astype(jnp.bfloat16)

    def take_right(which, number):
        all_right(which, 0, number).wait_recv()
        gather_sums(right_in.at[which], right_all.at[which], 0, 1)

    def take_left(which):
        local = jnp.logical_and(holds_left, which == slot)

        @pl.when(local)
        def _():
            all_left(which, 0, plane - 1).wait_recv()

        @pl.when(jnp.logical_not(local))
        def _():
            all_left(which, 0, plane).wait_recv()

        gather_sums(left_in.at[which], left_all, 0, 1)

    take_right(slot, plane - 1)
    take_right(slot_beside, plane)

    def tri_copy(which, index):
        return pltpu.make_async_remote_copy(
            src_ref=tri_out.at[which, index],
            dst_ref=tri_in.at[me],
            send_sem=tri_send,
            recv_sem=tri_recv,
            device_id=at(first + which, owner0 + index),
            device_id_type=MESH,
        )

    def is_mine(which, index):
        return jnp.logical_and(first + which == x, owner0 + index == me)

    low_lanes = lax.broadcasted_iota(jnp.int32, (block, LANES), 1) < owners * width
    for which in range(half):
        take_left(which)
        for c in range(block):
            triangle = lax.dot_general(
                left_all[c],
                right_all[:, c].reshape(half * rows, LANES),
                (((1,), (1,)), ((), ())),
                preferred_element_type=jnp.float32,
            )
            spread[pl.ds(c, rows, stride=block + PAD), : half * rows] = triangle
        for q in range(tiles):
            at_row = [
                spread[pl.ds((q * per_tile + a) * (block + PAD), block), :] for a in range(per_tile)
            ]
            swapped = swap_groups(
                [
                    jnp.where(low_lanes, at_row[a], pltpu.roll(at_row[a + owners], owners * width, 1))
                    for a in range(owners)
                ],
                width,
            )
            for index in range(owners):
                tri_out[which, index, q] = swapped[index].astype(jnp.bfloat16)
        for index in range(owners):

            @pl.when(jnp.logical_not(is_mine(which, index)))
            def _():
                tri_copy(which, index).start()

            @pl.when(is_mine(which, index))
            def _():
                tri_in[me] = tri_out[which, index]

    for load in loads[6:]:
        load.wait()

    def all_sums(number):
        return all_of(tri_in, number, tri_in, tri_send, tri_recv)

    @pl.when(sums_here)
    def _():
        all_sums(plane - 1).wait_recv()

    @pl.when(jnp.logical_not(sums_here))
    def _():
        all_sums(plane).wait_recv()

    for q in range(tiles):
        lanes = slice(q * LANES, (q + 1) * LANES)
        sums = tri_in[:, q].reshape(hidden, LANES).astype(jnp.float32)
        centered = sums - jnp.mean(sums, axis=0, keepdims=True)
        variance = jnp.mean(centered * centered, axis=0, keepdims=True)
        scaled = (centered * lax.rsqrt(variance + EPSILON)).T
        tri_normed = (scaled * out_gain_ref[...] + out_bias_ref[...]).astype(jnp.bfloat16)
        mixed = jnp.dot(tri_normed, out_weight_ref[...], preferred_element_type=jnp.float32)
        out_ref[q * per_tile : (q + 1) * per_tile] = (
            (gating_ref[lanes, :] * mixed).astype(jnp.bfloat16).reshape(per_tile, width, channels)
        )

    all_right(0, 0, plane - 1).wait_send()
    all_right(0, 1, plane).wait_send()
    all_left(0, 1, plane).wait_send()

    @pl.when(holds_left)
    def _():
        all_left(0, 0, plane - 1).wait_send()

    @pl.when(jnp.logical_not(holds_left))
    def _():
        all_left(0, 0, plane).wait_send()

    @pl.when(sums_here)
    def _():
        all_sums(plane - 1).wait_send()

    @pl.when(jnp.logical_not(sums_here))
    def _():
        all_sums(plane).wait_send()


def fused(nx, ny, nz, *arguments):
    pair, pair_mask, in_gain, in_bias, proj_weight, gate_weight, out_gain, out_bias, out_weight = arguments
    rows, width, channels = pair.shape
    hidden = proj_weight.shape[1] // 4
    plane = ny * nz
    block = hidden // plane
    tiles = rows * width // LANES
    half = nx // 2
    owners = half * rows // width
    travelling = (tiles, block, LANES)
    dma = pltpu.SemaphoreType.DMA
    return pl.pallas_call(
        functools.partial(kernel, nx, ny, nz),
        out_shape=pltpu.VMEM(pair.shape, jnp.bfloat16),
        in_specs=[pl.BlockSpec(memory_space=pltpu.HBM)] * 9,
        out_specs=pl.BlockSpec(memory_space=pltpu.VMEM),
        scratch_shapes=[
            pltpu.VMEM((plane, *travelling), jnp.bfloat16),
            pltpu.VMEM((plane, *travelling), jnp.bfloat16),
            pltpu.VMEM((half, owners, *travelling), jnp.bfloat16),
            pltpu.VMEM((2, plane, *travelling), jnp.bfloat16),
            pltpu.VMEM((half, plane, *travelling), jnp.bfloat16),
            pltpu.VMEM((plane, *travelling), jnp.bfloat16),
            pltpu.VMEM((half, block, rows, LANES), jnp.bfloat16),
            pltpu.VMEM((block, rows, LANES), jnp.bfloat16),
            pltpu.VMEM(((block + PAD) * (rows + PAD), LANES), jnp.float32),
            pltpu.VMEM((rows * width, channels), jnp.bfloat16),
            pltpu.VMEM((rows * width, channels), jnp.float32),
            dma((2,)),
            dma((half,)),
            dma((2,)),
            dma((half,)),
            dma,
            dma,
            pltpu.VMEM(pair.shape, pair.dtype),
            pltpu.VMEM((width, rows), pair_mask.dtype),
            pltpu.VMEM((1, in_gain.size), in_gain.dtype),
            pltpu.VMEM((1, in_bias.size), in_bias.dtype),
            pltpu.VMEM(proj_weight.shape, proj_weight.dtype),
            pltpu.VMEM(gate_weight.shape, gate_weight.dtype),
            pltpu.VMEM((1, out_gain.size), out_gain.dtype),
            pltpu.VMEM((1, out_bias.size), out_bias.dtype),
            pltpu.VMEM(out_weight.shape, out_weight.dtype),
            dma((9,)),
        ],
        compiler_params=pltpu.CompilerParams(collective_id=0, has_side_effects=True),
    )(
        pair,
        pair_mask.T,
        in_gain.reshape(1, -1),
        in_bias.reshape(1, -1),
        proj_weight,
        gate_weight,
        out_gain.reshape(1, -1),
        out_bias.reshape(1, -1),
        out_weight,
    )


def solution(mesh):
    nx, ny, nz = mesh.shape["gx"], mesh.shape["gy"], mesh.shape["gz"]
    plane = ny * nz

    def on_device(pair, *others):
        rows, width, channels = pair.shape
        hidden = others[3].shape[1] // 4
        fits = (
            width * plane == LANES
            and rows * nx == LANES
            and rows % width == 0
            and rows * width % (RIGHT_STEPS * LANES) == 0
            and nx == 4
            and channels % LANES == 0
            and hidden % (16 * plane) == 0
        )
        if fits:
            return fused(nx, ny, nz, pair, *others)
        return with_collectives(pair, *others)

    return jax.shard_map(
        on_device,
        mesh=mesh,
        in_specs=(
            P("gx", ("gy", "gz"), None),
            P("gx", ("gy", "gz")),
            P(),
            P(),
            P(),
            P(),
            P(),
            P(),
            P(),
        ),
        out_specs=P("gx", ("gy", "gz"), None),
        check_vma=False,
    )
```

time: 22.6 us -> 19.7 us (0.87)
  the two profiles are of different devices: /device:TPU:0 before, /device:TPU:25 now
where the time goes in v2:
time: 19.7 us; the launch traced here: 19.6 us
  Pallas kernels  18.9 us (96%)
  local copies, waits for them, and re-layouts  0.66 us (3%)
    pallas_call x1, Pallas kernels, fused(): pl.pallas_call(functools.partial(kernel, nx, ny, nz), out_shape=pltpu.VME...  18.9 us
    unnamed x1, local copies, waits for them, and re-layouts  0.66 us

profile of v2, /device:TPU:25, one launch (start us, length us, event | category | flops | bytes accessed | tf_op | source)
XLA Modules:
  0.0 19.6 jit_solution(1399629369431528883)
XLA Ops:
  0.0 18.9 %shard_map.91 = bf16[32,16,128]{2,1,0:T(8,128)(2,1)S(1)} custom-call(bf16[32,16,128]{2,1,0:T(8,128)(2,1)} %pair_hbm.1, s32[16,32]{1,0:T(8,128)} %bitcast.5, f32[1,128]{1,0:T(1,128)} %bitcast.6, f32[1,128]{1,0:T(1,128)} %bitcast.7, bf16[128,512]{1,0:T(8,128)(2,1)} %proj_hbm.1, bf16[128,128]{1,0:T(8,128)(2,1)} %gate_hbm.1, f32[1,128]{1,0:T(1,128)} %bitcast.8, ...), custom_call_target="tpu_custom_call" | custom-call | tf_op jit(solution)/shard_map/pallas_call | solution.py:452
  18.9 0.7 %copy.11 = bf16[32,16,128]{2,1,0:T(8,128)(2,1)} copy(bf16[32,16,128]{2,1,0:T(8,128)(2,1)S(1)} %shard_map.91) | data formatting | bytes 262144

commit v3 on v2

--- a/solution.py
+++ b/solution.py
@@ -10,7 +10,7 @@
 MESH = pl.DeviceIdType.MESH
 LANES = 128
 EPSILON = 1e-05
-RIGHT_STEPS = 2
+CUTS = 2
 PAD = 1
 
 
@@ -100,6 +100,7 @@
     right_all,
     left_all,
     spread,
+    sums_at,
     normed_ref,
     gating_ref,
     right_send,
@@ -125,6 +126,8 @@
     block = hidden // plane
     tiles = rows * width // LANES
     per_tile = rows // tiles
+    cut = block // CUTS
+    part = hidden // CUTS
     half = nx // 2
     owners = half * rows // width
     x, y, z = lax.axis_index("gx"), lax.axis_index("gy"), lax.axis_index("gz")
@@ -181,15 +184,9 @@
     for load in (loads[0], loads[2], loads[3]):
         load.wait()
 
-    def norm(step):
-        some = slice(step * rows // RIGHT_STEPS, (step + 1) * rows // RIGHT_STEPS)
-        pairs = slice(some.start * width, some.stop * width)
-        normed_ref[pairs, :] = normalize(
-            pair_ref[some].reshape(-1, channels).astype(jnp.float32), in_gain_ref[...], in_bias_ref[...]
-        ).astype(jnp.bfloat16)
-
-    norm(0)
-
+    normed_ref[...] = normalize(
+        pair_ref[...].reshape(-1, channels).astype(jnp.float32), in_gain_ref[...], in_bias_ref[...]
+    ).astype(jnp.bfloat16)
     loads[1].wait()
     row_of = lax.broadcasted_iota(jnp.int32, (rows, rows * width), 1) // width
     choose = (row_of == lax.broadcasted_iota(jnp.int32, row_of.shape, 0)).astype(jnp.bfloat16)
@@ -200,156 +197,148 @@
     own_column = column_of == lax.broadcasted_iota(jnp.int32, repeated.shape, 0)
     mask_row = jnp.sum(jnp.where(own_column, repeated, 0.0), axis=0, keepdims=True)
 
-    def side(weight, target, step, steps):
-        for q in range(step * tiles // steps, (step + 1) * tiles // steps):
+    def side(base, target, h):
+        gates = proj_ref[:, base + h * part : base + (h + 1) * part]
+        values = proj_ref[:, base + hidden + h * part : base + hidden + (h + 1) * part]
+        weight = jnp.concatenate([gates, values], axis=1).T
+        for q in range(tiles):
             lanes = slice(q * LANES, (q + 1) * LANES)
             projected = lax.dot_general(
                 weight, normed_ref[lanes, :], (((1,), (1,)), ((), ())), preferred_element_type=jnp.float32
             )
-            value = jax.nn.sigmoid(projected[:hidden]) * projected[hidden:] * mask_row[:, lanes]
-            target[:, q] = value.astype(jnp.bfloat16).reshape(plane, block, LANES)
-
-    def part_of(step, steps):
-        return pl.ds(step * tiles // steps, tiles // steps)
-
-    def right_copy(far, step, t):
+            value = jax.nn.sigmoid(projected[:part]) * projected[part:] * mask_row[:, lanes]
+            target[h, :, q] = value.astype(jnp.bfloat16).reshape(plane, cut, LANES)
+
+    def right_copy(far, h, t):
         d = turn(t)
         return pltpu.make_async_remote_copy(
-            src_ref=right_out.at[d, part_of(step, RIGHT_STEPS)],
-            dst_ref=right_in.at[slot, me, part_of(step, RIGHT_STEPS)],
+            src_ref=right_out.at[h, d],
+            dst_ref=right_in.at[slot, h, me],
             send_sem=right_send.at[far],
-            recv_sem=right_recv.at[slot],
+            recv_sem=right_recv.at[slot, h],
             device_id=at(beside if far else x, d),
             device_id_type=MESH,
         )
 
-    def left_copy(far, t):
+    def left_copy(far, h, t):
         d = turn(t)
         return pltpu.make_async_remote_copy(
-            src_ref=left_out.at[d],
-            dst_ref=left_in.at[slot, me],
+            src_ref=left_out.at[h, d],
+            dst_ref=left_in.at[slot, h, me],
             send_sem=left_send.at[far],
-            recv_sem=left_recv.at[slot],
+            recv_sem=left_recv.at[slot, h],
             device_id=at(across if far else near, d),
             device_id_type=MESH,
         )
 
-    def all_of(held, number, target, send_sem, recv_sem):
-        return pltpu.make_async_remote_copy(
-            src_ref=held.at[pl.ds(0, number)],
-            dst_ref=target.at[pl.ds(0, number)],
-            send_sem=send_sem,
-            recv_sem=recv_sem,
+    def arrived(target, sem, number):
+        whole = target.at[pl.ds(0, number)]
+        pltpu.make_async_remote_copy(
+            src_ref=whole,
+            dst_ref=whole,
+            send_sem=tri_send,
+            recv_sem=sem,
             device_id=at(beside, me),
             device_id_type=MESH,
-        )
-
-    def all_right(which, far, number):
-        return all_of(right_out, number, right_in.at[which], right_send.at[far], right_recv.at[which])
-
-    def all_left(which, far, number):
-        return all_of(left_out, number, left_in.at[which], left_send.at[far], left_recv.at[which])
-
-    def send_right(far):
-        for step in range(RIGHT_STEPS):
-            for t in range(0 if far else 1, plane):
-                right_copy(far, step, t).start()
-
-    def send_left(far):
+        ).wait_recv()
+
+    def departed(held, sem, number):
+        whole = held.at[:, pl.ds(0, number)]
+        pltpu.make_async_remote_copy(
+            src_ref=whole,
+            dst_ref=whole,
+            send_sem=sem,
+            recv_sem=tri_recv.at[0],
+            device_id=at(beside, me),
+            device_id_type=MESH,
+        ).wait_send()
+
+    def send_right(far, h):
+        for t in range(0 if far else 1, plane):
+            right_copy(far, h, t).start()
+
+    def send_left(far, h):
         for t in range(1, plane):
-            left_copy(far, t).start()
+            left_copy(far, h, t).start()
         if far:
-            left_copy(far, 0).start()
+            left_copy(far, h, 0).start()
         else:
 
             @pl.when(jnp.logical_not(holds_left))
             def _():
-                left_copy(far, 0).start()
+                left_copy(far, h, 0).start()
 
     def all_greeted():
         pl.semaphore_wait(barrier, 3 * plane - 1)
 
     loads[4].wait()
-    right_weight = proj_ref[:, 2 * hidden :].T
-    for step in range(RIGHT_STEPS):
-        if step > 0:
-            norm(step)
-        side(right_weight, right_out, step, RIGHT_STEPS)
-
-    @pl.when(x == last)
-    def _():
-        all_greeted()
-        send_right(1)
-
-    side(proj_ref[:, : 2 * hidden].T, left_out, 0, 1)
-
-    @pl.when(x != last)
-    def _():
-        all_greeted()
-
-    @pl.when(x == half)
-    def _():
-        send_right(0)
-
-    send_left(1)
-
-    @pl.when(x != last)
-    def _():
-        send_right(1)
-
-    @pl.when(x != half)
-    def _():
-        send_right(0)
-
-    send_left(0)
-    right_in[slot, me] = right_out[me]
-
-    @pl.when(holds_left)
-    def _():
-        left_in[slot, me] = left_out[me]
+    for h in range(CUTS):
+        side(2 * hidden, right_out, h)
+
+        @pl.when(x == last)
+        def _():
+            if h == 0:
+                all_greeted()
+            send_right(1, h)
+
+        side(0, left_out, h)
+
+        @pl.when(x != last)
+        def _():
+            if h == 0:
+                all_greeted()
+
+        @pl.when(x == half)
+        def _():
+            send_right(0, h)
+
+        send_left(1, h)
+
+        @pl.when(x != last)
+        def _():
+            send_right(1, h)
+
+        @pl.when(x != half)
+        def _():
+            send_right(0, h)
+
+        send_left(0, h)
+        right_in[slot, h, me] = right_out[h, me]
+
+        @pl.when(holds_left)
+        def _():
+            left_in[slot, h, me] = left_out[h, me]
 
     loads[5].wait()
     gating_ref[...] = jax.nn.sigmoid(
         jnp.dot(normed_ref[...], gate_ref[...], preferred_element_type=jnp.float32)
     )
 
-    def gather_sums(source, target, step, steps):
-        some = rows // steps
-        for index, q in enumerate(range(step * tiles // steps, (step + 1) * tiles // steps)):
+    def gather_sums(source, target, at_rows):
+        for q in range(tiles):
             swapped = swap_groups([source[a, q].astype(jnp.float32) for a in range(plane)], width)
             for a in range(per_tile):
-                spread[pl.ds(index * per_tile + a, block, stride=some + PAD), :] = swapped[a]
-        for c in range(block):
-            target[c, step * some : (step + 1) * some] = spread[
-                pl.ds(c * (some + PAD), some), :
-            ].astype(jnp.bfloat16)
-
-    def take_right(which, number):
-        all_right(which, 0, number).wait_recv()
-        gather_sums(right_in.at[which], right_all.at[which], 0, 1)
-
-    def take_left(which):
+                at_rows[pl.ds(q * per_tile + a, cut, stride=rows + PAD), :] = swapped[a]
+        for c in range(cut):
+            target[c] = at_rows[pl.ds(c * (rows + PAD), rows), :].astype(jnp.bfloat16)
+
+    def left_arrived(which, h):
         local = jnp.logical_and(holds_left, which == slot)
 
         @pl.when(local)
         def _():
-            all_left(which, 0, plane - 1).wait_recv()
+            arrived(left_in.at[which, h], left_recv.at[which, h], plane - 1)
 
         @pl.when(jnp.logical_not(local))
         def _():
-            all_left(which, 0, plane).wait_recv()
-
-        gather_sums(left_in.at[which], left_all, 0, 1)
-
-    take_right(slot, plane - 1)
-    take_right(slot_beside, plane)
-
-    def tri_copy(which, index):
+            arrived(left_in.at[which, h], left_recv.at[which, h], plane)
+
+    def tri_copy(which, h, index):
         return pltpu.make_async_remote_copy(
-            src_ref=tri_out.at[which, index],
-            dst_ref=tri_in.at[me],
+            src_ref=tri_out.at[h, which, index],
+            dst_ref=tri_in.at[h, me],
             send_sem=tri_send,
-            recv_sem=tri_recv,
+            recv_sem=tri_recv.at[h],
             device_id=at(first + which, owner0 + index),
             device_id_type=MESH,
         )
@@ -357,57 +346,67 @@
     def is_mine(which, index):
         return jnp.logical_and(first + which == x, owner0 + index == me)
 
-    low_lanes = lax.broadcasted_iota(jnp.int32, (block, LANES), 1) < owners * width
-    for which in range(half):
-        take_left(which)
-        for c in range(block):
+    low_lanes = lax.broadcasted_iota(jnp.int32, (cut, LANES), 1) < owners * width
+    for h in range(CUTS):
+        arrived(right_in.at[slot, h], right_recv.at[slot, h], plane - 1)
+        arrived(right_in.at[slot_beside, h], right_recv.at[slot_beside, h], plane)
+        for which in range(half):
+            left_arrived(which, h)
+        for which in range(half):
+            gather_sums(right_in.at[which, h], right_all.at[which], spread.at[which])
+            gather_sums(left_in.at[which, h], left_all.at[which], spread.at[half + which])
+        for c in range(cut):
             triangle = lax.dot_general(
-                left_all[c],
+                left_all[:, c].reshape(half * rows, LANES),
                 right_all[:, c].reshape(half * rows, LANES),
                 (((1,), (1,)), ((), ())),
                 preferred_element_type=jnp.float32,
             )
-            spread[pl.ds(c, rows, stride=block + PAD), : half * rows] = triangle
-        for q in range(tiles):
-            at_row = [
-                spread[pl.ds((q * per_tile + a) * (block + PAD), block), :] for a in range(per_tile)
-            ]
-            swapped = swap_groups(
-                [
-                    jnp.where(low_lanes, at_row[a], pltpu.roll(at_row[a + owners], owners * width, 1))
-                    for a in range(owners)
-                ],
-                width,
-            )
+            for which in range(half):
+                sums_at[which, pl.ds(c, rows, stride=cut + PAD), : half * rows] = triangle[
+                    which * rows : (which + 1) * rows
+                ]
+        for which in range(half):
+            for q in range(tiles):
+                at_row = [
+                    sums_at[which, pl.ds((q * per_tile + a) * (cut + PAD), cut), :] for a in range(per_tile)
+                ]
+                swapped = swap_groups(
+                    [
+                        jnp.where(low_lanes, at_row[a], pltpu.roll(at_row[a + owners], owners * width, 1))
+                        for a in range(owners)
+                    ],
+                    width,
+                )
+                for index in range(owners):
+                    tri_out[h, which, index, q] = swapped[index].astype(jnp.bfloat16)
+        for which in range(half):
             for index in range(owners):
-                tri_out[which, index, q] = swapped[index].astype(jnp.bfloat16)
-        for index in range(owners):
-
-            @pl.when(jnp.logical_not(is_mine(which, index)))
-            def _():
-                tri_copy(which, index).start()
-
-            @pl.when(is_mine(which, index))
-            def _():
-                tri_in[me] = tri_out[which, index]
+
+                @pl.when(jnp.logical_not(is_mine(which, index)))
+                def _():
+                    tri_copy(which, h, index).start()
+
+                @pl.when(is_mine(which, index))
+                def _():
+                    tri_in[h, me] = tri_out[h, which, index]
 
     for load in loads[6:]:
         load.wait()
 
-    def all_sums(number):
-        return all_of(tri_in, number, tri_in, tri_send, tri_recv)
-
     @pl.when(sums_here)
     def _():
-        all_sums(plane - 1).wait_recv()
+        for h in range(CUTS):
+            arrived(tri_in.at[h], tri_recv.at[h], plane - 1)
 
     @pl.when(jnp.logical_not(sums_here))
     def _():
-        all_sums(plane).wait_recv()
+        for h in range(CUTS):
+            arrived(tri_in.at[h], tri_recv.at[h], plane)
 
     for q in range(tiles):
         lanes = slice(q * LANES, (q + 1) * LANES)
-        sums = tri_in[:, q].reshape(hidden, LANES).astype(jnp.float32)
+        sums = tri_in[:, :, q].astype(jnp.float32).reshape(hidden, LANES)
         centered = sums - jnp.mean(sums, axis=0, keepdims=True)
         variance = jnp.mean(centered * centered, axis=0, keepdims=True)
         scaled = (centered * lax.rsqrt(variance + EPSILON)).T
@@ -417,25 +416,25 @@
             (gating_ref[lanes, :] * mixed).astype(jnp.bfloat16).reshape(per_tile, width, channels)
         )
 
-    all_right(0, 0, plane - 1).wait_send()
-    all_right(0, 1, plane).wait_send()
-    all_left(0, 1, plane).wait_send()
+    departed(right_out, right_send.at[0], plane - 1)
+    departed(right_out, right_send.at[1], plane)
+    departed(left_out, left_send.at[1], plane)
 
     @pl.when(holds_left)
     def _():
-        all_left(0, 0, plane - 1).wait_send()
+        departed(left_out, left_send.at[0], plane - 1)
 
     @pl.when(jnp.logical_not(holds_left))
     def _():
-        all_left(0, 0, plane).wait_send()
+        departed(left_out, left_send.at[0], plane)
 
     @pl.when(sums_here)
     def _():
-        all_sums(plane - 1).wait_send()
+        departed(tri_in, tri_send, plane - 1)
 
     @pl.when(jnp.logical_not(sums_here))
     def _():
-        all_sums(plane).wait_send()
+        departed(tri_in, tri_send, plane)
 
 
 def fused(nx, ny, nz, *arguments):
@@ -447,7 +446,8 @@
     tiles = rows * width // LANES
     half = nx // 2
     owners = half * rows // width
-    travelling = (tiles, block, LANES)
+    cut = block // CUTS
+    travelling = (plane, tiles, cut, LANES)
     dma = pltpu.SemaphoreType.DMA
     return pl.pallas_call(
         functools.partial(kernel, nx, ny, nz),
@@ -455,23 +455,24 @@
         in_specs=[pl.BlockSpec(memory_space=pltpu.HBM)] * 9,
         out_specs=pl.BlockSpec(memory_space=pltpu.VMEM),
         scratch_shapes=[
-            pltpu.VMEM((plane, *travelling), jnp.bfloat16),
-            pltpu.VMEM((plane, *travelling), jnp.bfloat16),
-            pltpu.VMEM((half, owners, *travelling), jnp.bfloat16),
-            pltpu.VMEM((2, plane, *travelling), jnp.bfloat16),
-            pltpu.VMEM((half, plane, *travelling), jnp.bfloat16),
-            pltpu.VMEM((plane, *travelling), jnp.bfloat16),
-            pltpu.VMEM((half, block, rows, LANES), jnp.bfloat16),
-            pltpu.VMEM((block, rows, LANES), jnp.bfloat16),
-            pltpu.VMEM(((block + PAD) * (rows + PAD), LANES), jnp.float32),
+            pltpu.VMEM((CUTS, *travelling), jnp.bfloat16),
+            pltpu.VMEM((CUTS, *travelling), jnp.bfloat16),
+            pltpu.VMEM((CUTS, half, owners, *travelling[1:]), jnp.bfloat16),
+            pltpu.VMEM((half, CUTS, *travelling), jnp.bfloat16),
+            pltpu.VMEM((half, CUTS, *travelling), jnp.bfloat16),
+            pltpu.VMEM((CUTS, *travelling), jnp.bfloat16),
+            pltpu.VMEM((half, cut, rows, LANES), jnp.bfloat16),
+            pltpu.VMEM((half, cut, rows, LANES), jnp.bfloat16),
+            pltpu.VMEM((2 * half, cut * (rows + PAD), LANES), jnp.float32),
+            pltpu.VMEM((half, rows * (cut + PAD), LANES), jnp.float32),
             pltpu.VMEM((rows * width, channels), jnp.bfloat16),
             pltpu.VMEM((rows * width, channels), jnp.float32),
             dma((2,)),
-            dma((half,)),
+            dma((half, CUTS)),
             dma((2,)),
-            dma((half,)),
+            dma((half, CUTS)),
             dma,
-            dma,
+            dma((CUTS,)),
             pltpu.VMEM(pair.shape, pair.dtype),
             pltpu.VMEM((width, rows), pair_mask.dtype),
             pltpu.VMEM((1, in_gain.size), in_gain.dtype),
@@ -508,10 +509,10 @@
             width * plane == LANES
             and rows * nx == LANES
             and rows % width == 0
-            and rows * width % (RIGHT_STEPS * LANES) == 0
+            and rows * width % LANES == 0
             and nx == 4
             and channels % LANES == 0
-            and hidden % (16 * plane) == 0
+            and hidden % (8 * CUTS * plane) == 0
         )
         if fits:
             return fused(nx, ny, nz, pair, *others)

time: 19.7 us -> 19.2 us (0.975)
  the two profiles are of different devices: /device:TPU:25 before, /device:TPU:0 now
where the time goes in v3:
time: 19.2 us; the launch traced here: 19.1 us
  Pallas kernels  18.4 us (96%)
  local copies, waits for them, and re-layouts  0.66 us (3%)
    pallas_call x1, Pallas kernels, fused(): pl.pallas_call(functools.partial(kernel, nx, ny, nz), out_shape=pltpu.VME...  18.4 us
    unnamed x1, local copies, waits for them, and re-layouts  0.66 us

profile of v3, /device:TPU:0, one launch (start us, length us, event | category | flops | bytes accessed | tf_op | source)
XLA Modules:
  0.0 19.1 jit_solution(3465994495914441989)
XLA Ops:
  0.0 18.4 %shard_map.91 = bf16[32,16,128]{2,1,0:T(8,128)(2,1)S(1)} custom-call(bf16[32,16,128]{2,1,0:T(8,128)(2,1)} %pair_hbm.1, s32[16,32]{1,0:T(8,128)} %bitcast.5, f32[1,128]{1,0:T(1,128)} %bitcast.6, f32[1,128]{1,0:T(1,128)} %bitcast.7, bf16[128,512]{1,0:T(8,128)(2,1)} %proj_hbm.1, bf16[128,128]{1,0:T(8,128)(2,1)} %gate_hbm.1, f32[1,128]{1,0:T(1,128)} %bitcast.8, ...), custom_call_target="tpu_custom_call" | custom-call | tf_op jit(solution)/shard_map/pallas_call | solution.py:452
  18.4 0.7 %copy.11 = bf16[32,16,128]{2,1,0:T(8,128)(2,1)} copy(bf16[32,16,128]{2,1,0:T(8,128)(2,1)S(1)} %shard_map.91) | data formatting | bytes 262144

commit v4 on v3

--- a/solution.py
+++ b/solution.py
@@ -109,6 +109,7 @@
     left_recv,
     tri_send,
     tri_recv,
+    above_in,
     pair_ref,
     mask_ref,
     in_gain_ref,
@@ -150,6 +151,26 @@
     def turn(t):
         return lax.rem(me + t, plane)
 
+    barrier = pltpu.get_barrier_semaphore()
+
+    def greet(row, start):
+        for t in range(start, plane):
+            pl.semaphore_signal(barrier, inc=1, device_id=at(row, turn(t)), device_id_type=MESH)
+
+    @pl.when(x < half)
+    def _():
+        greet(x + 1, 0)
+
+    @pl.when(x == half)
+    def _():
+        greet(x - 1, 0)
+
+    @pl.when(is_inner)
+    def _():
+        greet(last, 0)
+
+    greet(x, 1)
+
     arguments = (
         (pair_hbm, pair_ref),
         (mask_hbm, mask_ref),
@@ -167,20 +188,6 @@
     ]
     for load in loads:
         load.start()
-    barrier = pltpu.get_barrier_semaphore()
-
-    def greet(row, start):
-        for t in range(start, plane):
-            pl.semaphore_signal(barrier, inc=1, device_id=at(row, turn(t)), device_id_type=MESH)
-
-    @pl.when(is_inner)
-    def _():
-        greet(across, 0)
-        greet(jnp.where(x < half, last, 0), 0)
-
-    greet(beside, 0)
-    greet(x, 1)
-
     for load in (loads[0], loads[2], loads[3]):
         load.wait()
 
@@ -269,40 +276,91 @@
                 left_copy(far, h, 0).start()
 
     def all_greeted():
-        pl.semaphore_wait(barrier, 3 * plane - 1)
+        others = jnp.where(x == 0, 0, jnp.where(x == half, 1, 2))
+        pl.semaphore_wait(barrier, plane - 1 + plane * others)
+
+    def tell():
+        pl.semaphore_signal(above_in, inc=1, device_id=at(x - 1, me), device_id_type=MESH)
+
+    def told():
+        pl.semaphore_wait(above_in, 1)
 
     loads[4].wait()
+    side(2 * hidden, right_out, 0)
+
+    @pl.when(x == last)
+    def _():
+        all_greeted()
+        tell()
+        send_right(1, 0)
+
+    side(0, left_out, 0)
+
+    @pl.when(x == 0)
+    def _():
+        all_greeted()
+        send_right(0, 0)
+        send_left(0, 0)
+
+    @pl.when(x == half - 1)
+    def _():
+        all_greeted()
+        tell()
+        send_left(1, 0)
+        send_left(0, 0)
+        send_right(0, 0)
+        send_right(1, 0)
+
+    @pl.when(x == half)
+    def _():
+        all_greeted()
+        send_right(0, 0)
+        send_left(1, 0)
+
+    @pl.when(x == last)
+    def _():
+        send_left(1, 0)
+        send_right(0, 0)
+        send_left(0, 0)
+
+    side(2 * hidden, right_out, 1)
+    side(0, left_out, 1)
+
+    @pl.when(x == 0)
+    def _():
+        send_right(0, 1)
+        send_left(0, 1)
+        told()
+        send_left(1, 0)
+        send_right(1, 0)
+        send_left(1, 1)
+        send_right(1, 1)
+
+    @pl.when(x == half - 1)
+    def _():
+        send_left(1, 1)
+        send_left(0, 1)
+        send_right(0, 1)
+        send_right(1, 1)
+
+    @pl.when(x == half)
+    def _():
+        send_right(0, 1)
+        send_left(1, 1)
+        told()
+        send_right(1, 0)
+        send_left(0, 0)
+        send_right(1, 1)
+        send_left(0, 1)
+
+    @pl.when(x == last)
+    def _():
+        send_right(1, 1)
+        send_left(1, 1)
+        send_right(0, 1)
+        send_left(0, 1)
+
     for h in range(CUTS):
-        side(2 * hidden, right_out, h)
-
-        @pl.when(x == last)
-        def _():
-            if h == 0:
-                all_greeted()
-            send_right(1, h)
-
-        side(0, left_out, h)
-
-        @pl.when(x != last)
-        def _():
-            if h == 0:
-                all_greeted()
-
-        @pl.when(x == half)
-        def _():
-            send_right(0, h)
-
-        send_left(1, h)
-
-        @pl.when(x != last)
-        def _():
-            send_right(1, h)
-
-        @pl.when(x != half)
-        def _():
-            send_right(0, h)
-
-        send_left(0, h)
         right_in[slot, h, me] = right_out[h, me]
 
         @pl.when(holds_left)
@@ -346,50 +404,62 @@
     def is_mine(which, index):
         return jnp.logical_and(first + which == x, owner0 + index == me)
 
-    low_lanes = lax.broadcasted_iota(jnp.int32, (cut, LANES), 1) < owners * width
+    lane = lax.broadcasted_iota(jnp.int32, (cut, LANES), 1)
+    fewer = owners // half
     for h in range(CUTS):
-        arrived(right_in.at[slot, h], right_recv.at[slot, h], plane - 1)
-        arrived(right_in.at[slot_beside, h], right_recv.at[slot_beside, h], plane)
         for which in range(half):
             left_arrived(which, h)
-        for which in range(half):
-            gather_sums(right_in.at[which, h], right_all.at[which], spread.at[which])
-            gather_sums(left_in.at[which, h], left_all.at[which], spread.at[half + which])
-        for c in range(cut):
-            triangle = lax.dot_general(
-                left_all[:, c].reshape(half * rows, LANES),
-                right_all[:, c].reshape(half * rows, LANES),
-                (((1,), (1,)), ((), ())),
-                preferred_element_type=jnp.float32,
-            )
+        for column in range(half):
+
+            @pl.when(slot == column)
+            def _():
+                arrived(right_in.at[column, h], right_recv.at[column, h], plane - 1)
+
+            @pl.when(slot != column)
+            def _():
+                arrived(right_in.at[column, h], right_recv.at[column, h], plane)
+
+            gather_sums(right_in.at[column, h], right_all.at[column], spread.at[column])
+            if column == 0:
+                for which in range(half):
+                    gather_sums(left_in.at[which, h], left_all.at[which], spread.at[half + which])
+            for c in range(cut):
+                triangle = lax.dot_general(
+                    left_all[:, c].reshape(half * rows, LANES),
+                    right_all[column, c],
+                    (((1,), (1,)), ((), ())),
+                    preferred_element_type=jnp.float32,
+                )
+                for which in range(half):
+                    sums_at[which, pl.ds(c, rows, stride=cut + PAD), :rows] = triangle[
+                        which * rows : (which + 1) * rows
+                    ]
             for which in range(half):
-                sums_at[which, pl.ds(c, rows, stride=cut + PAD), : half * rows] = triangle[
-                    which * rows : (which + 1) * rows
-                ]
-        for which in range(half):
-            for q in range(tiles):
-                at_row = [
-                    sums_at[which, pl.ds((q * per_tile + a) * (cut + PAD), cut), :] for a in range(per_tile)
-                ]
-                swapped = swap_groups(
-                    [
-                        jnp.where(low_lanes, at_row[a], pltpu.roll(at_row[a + owners], owners * width, 1))
-                        for a in range(owners)
-                    ],
-                    width,
-                )
-                for index in range(owners):
-                    tri_out[h, which, index, q] = swapped[index].astype(jnp.bfloat16)
-        for which in range(half):
-            for index in range(owners):
-
-                @pl.when(jnp.logical_not(is_mine(which, index)))
-                def _():
-                    tri_copy(which, h, index).start()
-
-                @pl.when(is_mine(which, index))
-                def _():
-                    tri_in[h, me] = tri_out[h, which, index]
+                for q in range(tiles):
+                    at_row = [
+                        sums_at[which, pl.ds((q * per_tile + a) * (cut + PAD), cut), :]
+                        for a in range(per_tile)
+                    ]
+                    packed = []
+                    for a in range(fewer):
+                        lanes_of = at_row[a]
+                        for g in range(1, per_tile // fewer):
+                            moved = pltpu.roll(at_row[a + g * fewer], g * fewer * width, 1)
+                            lanes_of = jnp.where(lane < g * fewer * width, lanes_of, moved)
+                        packed.append(lanes_of)
+                    swapped = swap_groups(packed, width)
+                    for index in range(fewer):
+                        tri_out[h, which, column * fewer + index, q] = swapped[index].astype(jnp.bfloat16)
+            for index in range(column * fewer, (column + 1) * fewer):
+                for which in range(half):
+
+                    @pl.when(jnp.logical_not(is_mine(which, index)))
+                    def _():
+                        tri_copy(which, h, index).start()
+
+                    @pl.when(is_mine(which, index))
+                    def _():
+                        tri_in[h, me] = tri_out[h, which, index]
 
     for load in loads[6:]:
         load.wait()
@@ -473,6 +543,7 @@
             dma((half, CUTS)),
             dma,
             dma((CUTS,)),
+            pltpu.SemaphoreType.REGULAR,
             pltpu.VMEM(pair.shape, pair.dtype),
             pltpu.VMEM((width, rows), pair_mask.dtype),
             pltpu.VMEM((1, in_gain.size), in_gain.dtype),

time: 19.2 us -> 18.4 us (0.958)
  the two profiles are of different devices: /device:TPU:0 before, /device:TPU:25 now
where the time goes in v4:
time: 18.4 us; the launch traced here: 18.2 us
  Pallas kernels  17.5 us (95%)
  local copies, waits for them, and re-layouts  0.66 us (4%)
    pallas_call x1, Pallas kernels, fused(): pl.pallas_call(functools.partial(kernel, nx, ny, nz), out_shape=pltpu.VME...  17.5 us
    unnamed x1, local copies, waits for them, and re-layouts  0.66 us

profile of v4, /device:TPU:25, one launch (start us, length us, event | category | flops | bytes accessed | tf_op | source)
XLA Modules:
  0.0 18.2 jit_solution(6187697021234997700)
XLA Ops:
  0.0 17.5 %shard_map.91 = bf16[32,16,128]{2,1,0:T(8,128)(2,1)S(1)} custom-call(bf16[32,16,128]{2,1,0:T(8,128)(2,1)} %pair_hbm.1, s32[16,32]{1,0:T(8,128)} %bitcast.5, f32[1,128]{1,0:T(1,128)} %bitcast.6, f32[1,128]{1,0:T(1,128)} %bitcast.7, bf16[128,512]{1,0:T(8,128)(2,1)} %proj_hbm.1, bf16[128,128]{1,0:T(8,128)(2,1)} %gate_hbm.1, f32[1,128]{1,0:T(1,128)} %bitcast.8, ...), custom_call_target="tpu_custom_call" | custom-call | tf_op jit(solution)/shard_map/pallas_call | solution.py:522
  17.6 0.7 %copy.11 = bf16[32,16,128]{2,1,0:T(8,128)(2,1)} copy(bf16[32,16,128]{2,1,0:T(8,128)(2,1)S(1)} %shard_map.91) | data formatting | bytes 262144

commit v5 on v4

--- a/solution.py
+++ b/solution.py
@@ -161,7 +161,7 @@
     def _():
         greet(x + 1, 0)
 
-    @pl.when(x == half)
+    @pl.when(jnp.logical_or(x == half, x == 1))
     def _():
         greet(x - 1, 0)
 
@@ -276,7 +276,7 @@
                 left_copy(far, h, 0).start()
 
     def all_greeted():
-        others = jnp.where(x == 0, 0, jnp.where(x == half, 1, 2))
+        others = jnp.where(lax.rem(x, 2) == 0, 1, 2)
         pl.semaphore_wait(barrier, plane - 1 + plane * others)
 
     def tell():
@@ -301,13 +301,14 @@
         all_greeted()
         send_right(0, 0)
         send_left(0, 0)
+        send_right(1, 0)
 
     @pl.when(x == half - 1)
     def _():
         all_greeted()
         tell()
+        send_left(0, 0)
         send_left(1, 0)
-        send_left(0, 0)
         send_right(0, 0)
         send_right(1, 0)
 
@@ -332,14 +333,13 @@
         send_left(0, 1)
         told()
         send_left(1, 0)
-        send_right(1, 0)
         send_left(1, 1)
         send_right(1, 1)
 
     @pl.when(x == half - 1)
     def _():
+        send_left(0, 1)
         send_left(1, 1)
-        send_left(0, 1)
         send_right(0, 1)
         send_right(1, 1)
 
@@ -355,8 +355,8 @@
 
     @pl.when(x == last)
     def _():
+        send_left(1, 1)
         send_right(1, 1)
-        send_left(1, 1)
         send_right(0, 1)
         send_left(0, 1)
 
@@ -409,24 +409,16 @@
     for h in range(CUTS):
         for which in range(half):
             left_arrived(which, h)
-        for column in range(half):
-
-            @pl.when(slot == column)
-            def _():
-                arrived(right_in.at[column, h], right_recv.at[column, h], plane - 1)
-
-            @pl.when(slot != column)
-            def _():
-                arrived(right_in.at[column, h], right_recv.at[column, h], plane)
-
-            gather_sums(right_in.at[column, h], right_all.at[column], spread.at[column])
-            if column == 0:
+        for turned, column in enumerate((slot, slot_beside)):
+            arrived(right_in.at[column, h], right_recv.at[column, h], plane - 1 if turned == 0 else plane)
+            gather_sums(right_in.at[column, h], right_all.at[turned], spread.at[turned])
+            if turned == 0:
                 for which in range(half):
                     gather_sums(left_in.at[which, h], left_all.at[which], spread.at[half + which])
             for c in range(cut):
                 triangle = lax.dot_general(
                     left_all[:, c].reshape(half * rows, LANES),
-                    right_all[column, c],
+                    right_all[turned, c],
                     (((1,), (1,)), ((), ())),
                     preferred_element_type=jnp.float32,
                 )
@@ -450,7 +442,7 @@
                     swapped = swap_groups(packed, width)
                     for index in range(fewer):
                         tri_out[h, which, column * fewer + index, q] = swapped[index].astype(jnp.bfloat16)
-            for index in range(column * fewer, (column + 1) * fewer):
+            for index in (column * fewer + one for one in range(fewer)):
                 for which in range(half):
 
                     @pl.when(jnp.logical_not(is_mine(which, index)))

time: 18.4 us -> 17.9 us (0.973)
  the two profiles are of different devices: /device:TPU:25 before, /device:TPU:0 now
where the time goes in v5:
time: 17.9 us; the launch traced here: 17.8 us
  Pallas kernels  17.1 us (96%)
  local copies, waits for them, and re-layouts  0.66 us (4%)
    pallas_call x1, Pallas kernels, fused(): pl.pallas_call(functools.partial(kernel, nx, ny, nz), out_shape=pltpu.VME...  17.1 us
    unnamed x1, local copies, waits for them, and re-layouts  0.66 us

profile of v5, /device:TPU:0, one launch (start us, length us, event | category | flops | bytes accessed | tf_op | source)
XLA Modules:
  0.0 17.8 jit_solution(458395280914646299)
XLA Ops:
  0.0 17.1 %shard_map.91 = bf16[32,16,128]{2,1,0:T(8,128)(2,1)S(1)} custom-call(bf16[32,16,128]{2,1,0:T(8,128)(2,1)} %pair_hbm.1, s32[16,32]{1,0:T(8,128)} %bitcast.5, f32[1,128]{1,0:T(1,128)} %bitcast.6, f32[1,128]{1,0:T(1,128)} %bitcast.7, bf16[128,512]{1,0:T(8,128)(2,1)} %proj_hbm.1, bf16[128,128]{1,0:T(8,128)(2,1)} %gate_hbm.1, f32[1,128]{1,0:T(1,128)} %bitcast.8, ...), custom_call_target="tpu_custom_call" | custom-call | tf_op jit(solution)/shard_map/pallas_call | solution.py:514
  17.1 0.7 %copy.11 = bf16[32,16,128]{2,1,0:T(8,128)(2,1)} copy(bf16[32,16,128]{2,1,0:T(8,128)(2,1)S(1)} %shard_map.91) | data formatting | bytes 262144

commit v6 on v5

--- a/solution.py
+++ b/solution.py
@@ -299,18 +299,17 @@
     @pl.when(x == 0)
     def _():
         all_greeted()
+        send_right(1, 0)
         send_right(0, 0)
         send_left(0, 0)
-        send_right(1, 0)
 
     @pl.when(x == half - 1)
     def _():
         all_greeted()
         tell()
+        send_left(1, 0)
         send_left(0, 0)
-        send_left(1, 0)
         send_right(0, 0)
-        send_right(1, 0)
 
     @pl.when(x == half)
     def _():
@@ -329,17 +328,18 @@
 
     @pl.when(x == 0)
     def _():
-        send_right(0, 1)
-        send_left(0, 1)
         told()
         send_left(1, 0)
         send_left(1, 1)
+        send_right(0, 1)
+        send_left(0, 1)
         send_right(1, 1)
 
     @pl.when(x == half - 1)
     def _():
+        send_left(1, 1)
         send_left(0, 1)
-        send_left(1, 1)
+        send_right(1, 0)
         send_right(0, 1)
         send_right(1, 1)
 
@@ -406,52 +406,68 @@
 
     lane = lax.broadcasted_iota(jnp.int32, (cut, LANES), 1)
     fewer = owners // half
-    for h in range(CUTS):
+
+    def sums_of(turned, h):
+        column = slot_beside if turned else slot
+        if turned == 0:
+            for which in range(half):
+                left_arrived(which, h)
+        arrived(right_in.at[column, h], right_recv.at[column, h], plane - 1 if turned == 0 else plane)
+        gather_sums(right_in.at[column, h], right_all.at[turned], spread.at[turned])
+        if turned == 0:
+            for which in range(half):
+                gather_sums(left_in.at[which, h], left_all.at[h, which], spread.at[half + which])
+        for c in range(cut):
+            triangle = lax.dot_general(
+                left_all[h, :, c].reshape(half * rows, LANES),
+                right_all[turned, c],
+                (((1,), (1,)), ((), ())),
+                preferred_element_type=jnp.float32,
+            )
+            for which in range(half):
+                sums_at[which, pl.ds(c, rows, stride=cut + PAD), :rows] = triangle[
+                    which * rows : (which + 1) * rows
+                ]
         for which in range(half):
-            left_arrived(which, h)
-        for turned, column in enumerate((slot, slot_beside)):
-            arrived(right_in.at[column, h], right_recv.at[column, h], plane - 1 if turned == 0 else plane)
-            gather_sums(right_in.at[column, h], right_all.at[turned], spread.at[turned])
-            if turned == 0:
-                for which in range(half):
-                    gather_sums(left_in.at[which, h], left_all.at[which], spread.at[half + which])
-            for c in range(cut):
-                triangle = lax.dot_general(
-                    left_all[:, c].reshape(half * rows, LANES),
-                    right_all[turned, c],
-                    (((1,), (1,)), ((), ())),
-                    preferred_element_type=jnp.float32,
-                )
-                for which in range(half):
-                    sums_at[which, pl.ds(c, rows, stride=cut + PAD), :rows] = triangle[
-                        which * rows : (which + 1) * rows
-                    ]
+            for q in range(tiles):
+                at_row = [
+                    sums_at[which, pl.ds((q * per_tile + a) * (cut + PAD), cut), :]
+                    for a in range(per_tile)
+                ]
+                packed = []
+                for a in range(fewer):
+                    lanes_of = at_row[a]
+                    for g in range(1, per_tile // fewer):
+                        moved = pltpu.roll(at_row[a + g * fewer], g * fewer * width, 1)
+                        lanes_of = jnp.where(lane < g * fewer * width, lanes_of, moved)
+                    packed.append(lanes_of)
+                swapped = swap_groups(packed, width)
+                for index in range(fewer):
+                    tri_out[h, which, column * fewer + index, q] = swapped[index].astype(jnp.bfloat16)
+        for index in (column * fewer + one for one in reversed(range(fewer))):
             for which in range(half):
-                for q in range(tiles):
-                    at_row = [
-                        sums_at[which, pl.ds((q * per_tile + a) * (cut + PAD), cut), :]
-                        for a in range(per_tile)
-                    ]
-                    packed = []
-                    for a in range(fewer):
-                        lanes_of = at_row[a]
-                        for g in range(1, per_tile // fewer):
-                            moved = pltpu.roll(at_row[a + g * fewer], g * fewer * width, 1)
-                            lanes_of = jnp.where(lane < g * fewer * width, lanes_of, moved)
-                        packed.append(lanes_of)
-                    swapped = swap_groups(packed, width)
-                    for index in range(fewer):
-                        tri_out[h, which, column * fewer + index, q] = swapped[index].astype(jnp.bfloat16)
-            for index in (column * fewer + one for one in range(fewer)):
-                for which in range(half):
-
-                    @pl.when(jnp.logical_not(is_mine(which, index)))
-                    def _():
-                        tri_copy(which, h, index).start()
-
-                    @pl.when(is_mine(which, index))
-                    def _():
-                        tri_in[h, me] = tri_out[h, which, index]
+
+                @pl.when(jnp.logical_not(is_mine(which, index)))
+                def _():
+                    tri_copy(which, h, index).start()
+
+                @pl.when(is_mine(which, index))
+                def _():
+                    tri_in[h, me] = tri_out[h, which, index]
+
+    sums_of(0, 0)
+
+    @pl.when(x == 0)
+    def _():
+        sums_of(0, 1)
+
+    sums_of(1, 0)
+
+    @pl.when(x != 0)
+    def _():
+        sums_of(0, 1)
+
+    sums_of(1, 1)
 
     for load in loads[6:]:
         load.wait()
@@ -524,7 +540,7 @@
             pltpu.VMEM((half, CUTS, *travelling), jnp.bfloat16),
             pltpu.VMEM((CUTS, *travelling), jnp.bfloat16),
             pltpu.VMEM((half, cut, rows, LANES), jnp.bfloat16),
-            pltpu.VMEM((half, cut, rows, LANES), jnp.bfloat16),
+            pltpu.VMEM((CUTS, half, cut, rows, LANES), jnp.bfloat16),
             pltpu.VMEM((2 * half, cut * (rows + PAD), LANES), jnp.float32),
             pltpu.VMEM((half, rows * (cut + PAD), LANES), jnp.float32),
             pltpu.VMEM((rows * width, channels), jnp.bfloat16),

time: 17.9 us -> 17.8 us (level)
  the two profiles are of different devices: /device:TPU:0 before, /device:TPU:6 now
where the time goes in v6:
time: 17.8 us; the launch traced here: 17.6 us
  Pallas kernels  16.9 us (95%)
  local copies, waits for them, and re-layouts  0.66 us (4%)
    pallas_call x1, Pallas kernels, fused(): pl.pallas_call(functools.partial(kernel, nx, ny, nz), out_shape=pltpu.VME...  16.9 us
    unnamed x1, local copies, waits for them, and re-layouts  0.66 us

profile of v6, /device:TPU:6, one launch (start us, length us, event | category | flops | bytes accessed | tf_op | source)
XLA Modules:
  0.0 17.6 jit_solution(3986560570839122134)
XLA Ops:
  0.0 16.9 %shard_map.91 = bf16[32,16,128]{2,1,0:T(8,128)(2,1)S(1)} custom-call(bf16[32,16,128]{2,1,0:T(8,128)(2,1)} %pair_hbm.1, s32[16,32]{1,0:T(8,128)} %bitcast.5, f32[1,128]{1,0:T(1,128)} %bitcast.6, f32[1,128]{1,0:T(1,128)} %bitcast.7, bf16[128,512]{1,0:T(8,128)(2,1)} %proj_hbm.1, bf16[128,128]{1,0:T(8,128)(2,1)} %gate_hbm.1, f32[1,128]{1,0:T(1,128)} %bitcast.8, ...), custom_call_target="tpu_custom_call" | custom-call | tf_op jit(solution)/shard_map/pallas_call | solution.py:530
  17.0 0.7 %copy.11 = bf16[32,16,128]{2,1,0:T(8,128)(2,1)} copy(bf16[32,16,128]{2,1,0:T(8,128)(2,1)S(1)} %shard_map.91) | data formatting | bytes 262144

commit v7 on v6

--- a/solution.py
+++ b/solution.py
@@ -444,8 +444,8 @@
                 swapped = swap_groups(packed, width)
                 for index in range(fewer):
                     tri_out[h, which, column * fewer + index, q] = swapped[index].astype(jnp.bfloat16)
-        for index in (column * fewer + one for one in reversed(range(fewer))):
-            for which in range(half):
+        for which in range(half):
+            for index in (column * fewer + one for one in reversed(range(fewer))):
 
                 @pl.when(jnp.logical_not(is_mine(which, index)))
                 def _():

time: 17.8 us -> 17.7 us (level)
  the two profiles are of different devices: /device:TPU:6 before, /device:TPU:5 now
where the time goes in v7:
time: 17.7 us; the launch traced here: 17.6 us
  Pallas kernels  16.9 us (95%)
  local copies, waits for them, and re-layouts  0.66 us (4%)
    pallas_call x1, Pallas kernels, fused(): pl.pallas_call(functools.partial(kernel, nx, ny, nz), out_shape=pltpu.VME...  16.9 us
    unnamed x1, local copies, waits for them, and re-layouts  0.66 us

profile of v7, /device:TPU:5, one launch (start us, length us, event | category | flops | bytes accessed | tf_op | source)
XLA Modules:
  0.0 17.6 jit_solution(12047685531242661205)
XLA Ops:
  0.0 16.9 %shard_map.91 = bf16[32,16,128]{2,1,0:T(8,128)(2,1)S(1)} custom-call(bf16[32,16,128]{2,1,0:T(8,128)(2,1)} %pair_hbm.1, s32[16,32]{1,0:T(8,128)} %bitcast.5, f32[1,128]{1,0:T(1,128)} %bitcast.6, f32[1,128]{1,0:T(1,128)} %bitcast.7, bf16[128,512]{1,0:T(8,128)(2,1)} %proj_hbm.1, bf16[128,128]{1,0:T(8,128)(2,1)} %gate_hbm.1, f32[1,128]{1,0:T(1,128)} %bitcast.8, ...), custom_call_target="tpu_custom_call" | custom-call | tf_op jit(solution)/shard_map/pallas_call | solution.py:530
  16.9 0.7 %copy.11 = bf16[32,16,128]{2,1,0:T(8,128)(2,1)} copy(bf16[32,16,128]{2,1,0:T(8,128)(2,1)S(1)} %shard_map.91) | data formatting | bytes 262144
